TPU v7x, 128 devices: a whole 4x4x4 slice. The times are simulated.
128 devices in a mesh: expert: 8 (over x, core), shard: 16 (over z, y).
Axes of the slice: x: 4, y: 4, z: 4, core: 2. Of those that a mesh axis runs over, the one named last changes fastest.
Arguments:
- tokens: bfloat16 [1024, 4096], P(('expert', 'shard')), may hold values from -6 to 6
- router: bfloat16 [4096, 8], replicated, may hold values from -0.09375 to 0.09375
- expert_ids: int32 [1024, 2], P(('expert', 'shard')), may hold values from 0 to 7, as said below
- w_gate: bfloat16 [8, 4096, 14336], P('expert', None, 'shard'), may hold values from -0.09375 to 0.09375
- w_up: bfloat16 [8, 4096, 14336], P('expert', None, 'shard'), may hold values from -0.09375 to 0.09375
- w_down: bfloat16 [8, 14336, 4096], P('expert', 'shard'), may hold values from -0.046875 to 0.046875
Outputs:
- mixed: bfloat16 [1024, 4096], P(('expert', 'shard'))
Inputs may be any that keep to these rules, and one draw needn't show every extreme that they name: `expert_ids`: each row names 2 different experts. Within the rows of one device no expert is named more than 4 times, and on every device some expert is named exactly 4 times.
All inputs are finite; a program needn't handle non-finite values.
Results may differ from a plain program's by a relative error of at most 0.0074.
Values may be sent and summed in bfloat16 or wider, within the bound.
A program may use at most 128 MiB of HBM per device.

v0:
```python
import jax
import jax.numpy as jnp
from jax import lax
from jax.sharding import PartitionSpec as P


def from_behind(value, axis, steps):
    count = lax.axis_size(axis)
    pairs = [(source, (source + steps) % count) for source in range(count)]
    return lax.ppermute(value, axis, pairs)


def laid_out(blocks, dim):
    blocks = jnp.moveaxis(blocks, 0, dim)
    dims = blocks.shape
    return blocks.reshape(*dims[:dim], dims[dim] * dims[dim + 1], *dims[dim + 2 :])


def work_in_pieces(x, axis, dim, apply, out_dim):
    devices, extent = (lax.axis_size(axis), x.shape[dim])
    count = 2 if extent % 2 == 0 else 1
    gathered, length = ([], extent // count)
    for k in range(count):
        share = lax.slice_in_dim(x, k * length, (k + 1) * length, axis=dim)
        starts = jnp.arange(devices) * extent + k * length
        gathered.append(jax.vmap(apply)(lax.all_gather(share, axis), starts))
    return laid_out(jnp.concatenate(gathered, axis=out_dim + 1), out_dim)


def split_up(x, dim, devices):
    before, after = (x.shape[:dim], x.shape[dim + 1 :])
    return jnp.moveaxis(x.reshape(*before, devices, -1, *after), dim, 0)


def sum_at_owner(x, axis, dim):
    devices = lax.axis_size(axis)
    blocks = lax.all_to_all(split_up(x, dim, devices), axis, 0, 0, tiled=True)
    return jnp.sum(blocks.astype(jnp.float32), axis=0)


def shards(tokens, router, expert_ids, w_gate, w_up, w_down):
    local_tokens = tokens.shape[0]
    width = tokens.shape[1]
    n_experts = router.shape[1]
    slots_per = local_tokens // 2
    half_slots = slots_per // 2
    shadow_gate, shadow_up, shadow_down = from_behind((w_gate, w_up, w_down), "expert", -1)
    logits = jnp.dot(tokens, router, preferred_element_type=jnp.float32)
    chosen = jnp.take_along_axis(logits, expert_ids, axis=1)
    first = 1.0 / (1.0 + jnp.exp(-(chosen[:, 0] - chosen[:, 1])))
    gates = jnp.stack([first, 1.0 - first], axis=1)
    flat_ids = expert_ids.reshape(-1)
    onehot = (flat_ids[:, None] == jnp.arange(n_experts, dtype=jnp.int32)[None, :]).astype(
        jnp.int32
    )
    before = jnp.cumsum(onehot, axis=0) - onehot
    slots = jnp.sum(before * onehot, axis=1)
    positions = flat_ids * slots_per + slots
    token_index = jnp.repeat(jnp.arange(local_tokens, dtype=jnp.int32), expert_ids.shape[1])
    outgoing = jnp.zeros((n_experts * slots_per, width), jnp.bfloat16)
    outgoing = outgoing.at[positions].set(tokens[token_index])
    outgoing = outgoing.reshape(n_experts, half_slots, 2, width)
    even_rows = outgoing[:, :, 0]
    odd_rows = jnp.roll(outgoing[:, :, 1], -1, axis=0)
    sending = jnp.stack([even_rows, odd_rows], axis=0)
    arrived = lax.all_to_all(sending, "expert", split_axis=1, concat_axis=1, tiled=True)
    arrived = arrived.reshape(2, n_experts * half_slots, width)
    gate_w = w_gate[0]
    up_w = w_up[0]
    down_w = w_down[0]
    gate_s = shadow_gate[0]
    up_s = shadow_up[0]
    down_s = shadow_down[0]

    def swiglu(rows, gate_m, up_m):
        gate = jnp.dot(rows, gate_m, preferred_element_type=jnp.float32)
        up = jnp.dot(rows, up_m, preferred_element_type=jnp.float32)
        return (jax.nn.silu(gate) * up).astype(jnp.bfloat16)

    def hidden_rows(piece, start):
        own = swiglu(piece[0], gate_w, up_w)
        other = swiglu(piece[1], gate_s, up_s)
        return jnp.stack([own, other], axis=1)

    hidden = work_in_pieces(arrived, "shard", 1, hidden_rows, 0)
    own = jnp.dot(hidden[:, 0], down_w, preferred_element_type=jnp.float32)
    other = jnp.dot(hidden[:, 1], down_s, preferred_element_type=jnp.float32)
    summed = sum_at_owner(jnp.stack([own, other], axis=1).astype(jnp.bfloat16), "shard", 0)
    finished = summed.astype(jnp.bfloat16).reshape(n_experts, half_slots, 2, width)
    returned = lax.all_to_all(finished, "expert", split_axis=0, concat_axis=0, tiled=True)
    even_back = returned[:, :, 0]
    odd_back = jnp.roll(returned[:, :, 1], 1, axis=0)
    by_expert = jnp.stack([even_back, odd_back], axis=2).reshape(n_experts * slots_per, width)
    picked = (
        by_expert[positions].reshape(local_tokens, expert_ids.shape[1], width).astype(jnp.float32)
    )
    mixed = jnp.sum(gates[:, :, None] * picked, axis=1)
    return mixed.astype(jnp.bfloat16)


def solution(mesh):
    placed = (
        P(("expert", "shard"), None),
        P(),
        P(("expert", "shard"), None),
        P("expert", None, "shard"),
        P("expert", None, "shard"),
        P("expert", "shard", None),
    )
    return jax.shard_map(
        shards, mesh=mesh, in_specs=placed, out_specs=P(("expert", "shard"), None), check_vma=False
    )
```

profile of v0, /device:TPU:1, one launch (start us, length us, event | category | flops | bytes accessed | tf_op | source)
XLA Modules:
  0.0 370.6 jit_solution(15408557589807152107)
XLA Ops:
  6.5 0.7 broadcast_multiply_fusion
  7.3 0.8 copy.103
  8.7 1.2 scatter_custom_fusion
  11.1 12.1 %all_to_all.15 = bf16[2,8,2,4096]{3,2,0,1:T(2,128)(2,1)S(1)} all-to-all(bf16[2,8,2,4096]{3,2,0,1:T(2,128)(2,1)S(1)} %copy.113), channel_id=1, replica_groups=mesh['expert'=8,'shard'=16] {'expert'}, dimensions={1} | all-to-all | bytes 524288 | tf_op jit(solution)/shard_map/all_to_all | solution.py:66
  23.7 0.7 copy.118
  24.6 1.1 collective-permute-start
  25.9 0.7 copy.115
  26.7 1.1 collective-permute-start.2
  27.7 41.2 %all-gather.7.cloned.1.call-done = bf16[32,8,4096]{2,1,0:T(8,128)(2,1)} async-done(((bf16[2,8,4096]{2,1,0:T(8,128)(2,1)}), bf16[32,8,4096]{2,1,0:T(8,128)(2,1)}) %all-gather.7.cloned.1.call-update) | async-done | bytes 2097168 | tf_op jit(solution)/shard_map/all_gather | solution.py:26
  69.0 4.7 %fusion.16 = f32[16,8,896]{2,1,0:T(8,128)S(1)} fusion(bf16[1,4096,896]{2,1,0:T(8,128)(2,1)} %param.9, bf16[16,2,8,4096]{3,2,1,0:T(8,128)(2,1)} %bitcast.140), kind=kOutput, calls=%fused_computation.20 | convolution fusion | flops 939524096 | bytes 8847360 | tf_op jit(solution)/shard_map/vmap()/dot_general | solution.py:76
  73.6 41.8 %all-gather.5.cloned.1.call-done = bf16[32,8,4096]{2,1,0:T(8,128)(2,1)} async-done(((bf16[2,8,4096]{2,1,0:T(8,128)(2,1)}), bf16[32,8,4096]{2,1,0:T(8,128)(2,1)}) %all-gather.5.cloned.1.call-update) | async-done | bytes 2097168 | tf_op jit(solution)/shard_map/all_gather | solution.py:26
  115.4 4.8 %fusion.18 = f32[16,8,896]{2,1,0:T(8,128)S(1)} fusion(bf16[1,4096,896]{2,1,0:T(8,128)(2,1)} %param.9, bf16[16,2,8,4096]{3,2,1,0:T(8,128)(2,1)} %bitcast.144), kind=kOutput, calls=%fused_computation.22 | convolution fusion | flops 939524096 | bytes 8847360 | tf_op jit(solution)/shard_map/vmap()/dot_general | solution.py:76
  120.3 4.5 %fusion.47 = bf16[16,8,1,896]{3,1,0,2:T(8,128)(2,1)S(1)} fusion(bf16[1,4096,896]{2,1,0:T(8,128)(2,1)} %param.10, bf16[16,2,8,4096]{3,2,1,0:T(8,128)(2,1)S(1)} %bitcast.141, f32[16,8,896]{2,1,0:T(8,128)S(1)} %fusion.16), kind=kOutput, calls=%fused_computation.34 | convolution fusion | flops 940212224 | bytes 9076736 | tf_op jit(solution)/shard_map/vmap()/dot_general | solution.py:77
  124.9 1.3 fusion.44
  126.2 4.4 %fusion.8 = f32[16,8,896]{2,1,0:T(8,128)S(1)} fusion(bf16[1,4096,896]{2,1,0:T(8,128)(2,1)} %collective-permute-done, bf16[16,2,8,4096]{3,2,1,0:T(8,128)(2,1)S(1)} %bitcast.142), kind=kOutput, calls=%fused_computation.12 | convolution fusion | flops 939524096 | bytes 8847360 | tf_op jit(solution)/shard_map/vmap()/dot_general | solution.py:76
  130.6 4.4 %fusion.10 = f32[16,8,896]{2,1,0:T(8,128)S(1)} fusion(bf16[1,4096,896]{2,1,0:T(8,128)(2,1)} %collective-permute-done, bf16[16,2,8,4096]{3,2,1,0:T(8,128)(2,1)S(1)} %bitcast.146), kind=kOutput, calls=%fused_computation.14 | convolution fusion | flops 939524096 | bytes 8847360 | tf_op jit(solution)/shard_map/vmap()/dot_general | solution.py:76
  135.0 50.3 %collective-permute-done.1 = bf16[1,4096,896]{2,1,0:T(8,128)(2,1)} collective-permute-done((bf16[1,4096,896]{2,1,0:T(8,128)(2,1)}, bf16[1,4096,896]{2,1,0:T(8,128)(2,1)}, u32[]{:S(2)}, u32[]{:S(2)}) %collective-permute-start.1) | collective-permute-done | bytes 7340064 | tf_op jit(solution)/shard_map/ppermute | solution.py:10
  185.2 4.5 %fusion.51 = bf16[16,8,1,896]{3,1,0,2:T(8,128)(2,1)S(1)} fusion(f32[16,8,896]{2,1,0:T(8,128)S(1)} %fusion.8, bf16[1,4096,896]{2,1,0:T(8,128)(2,1)} %collective-permute-done.1, bf16[16,2,8,4096]{3,2,1,0:T(8,128)(2,1)S(1)} %bitcast.143), kind=kOutput, calls=%fused_computation.46 | convolution fusion | flops 940212224 | bytes 9076736 | tf_op jit(solution)/shard_map/vmap()/dot_general | solution.py:77
  189.8 4.5 %fusion.50 = bf16[16,8,1,896]{3,1,0,2:T(8,128)(2,1)S(1)} fusion(f32[16,8,896]{2,1,0:T(8,128)S(1)} %fusion.10, bf16[1,4096,896]{2,1,0:T(8,128)(2,1)} %collective-permute-done.1, bf16[16,2,8,4096]{3,2,1,0:T(8,128)(2,1)S(1)} %bitcast.147), kind=kOutput, calls=%fused_computation.45 | convolution fusion | flops 940212224 | bytes 9076736 | tf_op jit(solution)/shard_map/vmap()/dot_general | solution.py:77
  194.5 2.6 fusion.29
  197.2 66.7 %collective-permute-done.2 = bf16[1,896,4096]{2,1,0:T(8,128)(2,1)} collective-permute-done((bf16[1,896,4096]{2,1,0:T(8,128)(2,1)}, bf16[1,896,4096]{2,1,0:T(8,128)(2,1)}, u32[]{:S(2)}, u32[]{:S(2)}) %collective-permute-start.2) | collective-permute-done | bytes 7340064 | tf_op jit(solution)/shard_map/ppermute | solution.py:10
  263.9 5.5 %fusion.26 = bf16[16,16,1,4096]{3,1,0,2:T(8,128)(2,1)S(1)} fusion(bf16[16,16,896]{2,1,0:T(8,128)(2,1)S(1)} %bitcast.153, bf16[1,896,4096]{2,1,0:T(8,128)(2,1)} %collective-permute-done.2), kind=kOutput, calls=%fused_computation.26 | convolution fusion | flops 1880096768 | bytes 9895936 | tf_op jit(solution)/shard_map/dot_general | solution.py:87
  269.8 2.2 copy.121
  272.0 8.0 %all-to-all-start.1 = ((bf16[16,16,2,4096]{3,1,2,0:T(8,128)(2,1)}), bf16[16,16,2,4096]{3,1,2,0:T(8,128)(2,1)}, u32[]{:S(2)}, u32[]{:S(2)}) async-start(bf16[16,16,2,4096]{3,1,2,0:T(8,128)(2,1)} %copy.121), calls=%async_computation.1 | async-start | bytes 8388608 | tf_op jit(solution)/shard_map/all_to_all | solution.py:37
  280.4 0.7 gather_fusion.1
  281.2 64.8 %all-to-all-done.1 = bf16[16,16,2,4096]{3,1,2,0:T(8,128)(2,1)} async-done(((bf16[16,16,2,4096]{3,1,2,0:T(8,128)(2,1)}), bf16[16,16,2,4096]{3,1,2,0:T(8,128)(2,1)}, u32[]{:S(2)}, u32[]{:S(2)}) %all-to-all-start.1) | async-done | bytes 4194336 | tf_op jit(solution)/shard_map/all_to_all | solution.py:37
  346.0 3.0 reduce_sum.34
  349.0 1.0 copy.123
  349.9 3.8 %all-to-all-start.2 = ((bf16[8,2,2,4096]{3,2,1,0:T(2,128)(2,1)}), bf16[8,2,2,4096]{3,2,1,0:T(2,128)(2,1)S(1)}, u32[]{:S(2)}, u32[]{:S(2)}) async-start(bf16[8,2,2,4096]{3,2,1,0:T(2,128)(2,1)} %bitcast.36), calls=%async_computation.2 | async-start | bytes 524288 | tf_op jit(solution)/shard_map/all_to_all | solution.py:90
  353.9 6.3 %all-to-all-done.2 = bf16[8,2,2,4096]{3,2,1,0:T(2,128)(2,1)S(1)} async-done(((bf16[8,2,2,4096]{3,2,1,0:T(2,128)(2,1)}), bf16[8,2,2,4096]{3,2,1,0:T(2,128)(2,1)S(1)}, u32[]{:S(2)}, u32[]{:S(2)}) %all-to-all-start.2) | async-done | bytes 262176 | tf_op jit(solution)/shard_map/all_to_all | solution.py:90
  361.9 0.6 gather_fusion
  362.7 1.0 multiply_reduce_fusion
  (68 shorter events, 5.8 us)
Async XLA Ops:
  6.5 2.1 copy-start
  6.5 62.4 %all-gather.7.cloned.1.call-start = ((), (), s32[]{:S(2)}) async-start(), calls=%async_computation.4 | async-start | bytes 2228224 | tf_op jit(solution)/shard_map/all_gather | solution.py:26
  24.4 91.0 %all-gather.5.cloned.1.call-start = ((), (), s32[]{:S(2)}) async-start(), calls=%async_computation.3 | async-start | bytes 2228224 | tf_op jit(solution)/shard_map/all_gather | solution.py:26
  24.6 101.6 %collective-permute-start = (bf16[1,4096,896]{2,1,0:T(8,128)(2,1)}, bf16[1,4096,896]{2,1,0:T(8,128)(2,1)}, u32[]{:S(2)}, u32[]{:S(2)}) collective-permute-start(bf16[1,4096,896]{2,1,0:T(8,128)(2,1)} %param.9), channel_id=1, source_target_pairs={{0,112},{16,0},{32,16},{48,32},{64,48},{80,64},{96,80},{112,96},{1... | collective-permute-start | bytes 22020104 | tf_op jit(solution)/shard_map/ppermute | solution.py:10
  25.7 159.6 %collective-permute-start.1 = (bf16[1,4096,896]{2,1,0:T(8,128)(2,1)}, bf16[1,4096,896]{2,1,0:T(8,128)(2,1)}, u32[]{:S(2)}, u32[]{:S(2)}) collective-permute-start(bf16[1,4096,896]{2,1,0:T(8,128)(2,1)} %param.10), channel_id=1, source_target_pairs={{0,112},{16,0},{32,16},{48,32},{64,48},{80,64},{96,80},{112,96},{1... | collective-permute-start | bytes 22020104 | tf_op jit(solution)/shard_map/ppermute | solution.py:10
  26.7 237.2 %collective-permute-start.2 = (bf16[1,896,4096]{2,1,0:T(8,128)(2,1)}, bf16[1,896,4096]{2,1,0:T(8,128)(2,1)}, u32[]{:S(2)}, u32[]{:S(2)}) collective-permute-start(bf16[1,896,4096]{2,1,0:T(8,128)(2,1)} %param.11), channel_id=1, source_target_pairs={{0,112},{16,0},{32,16},{48,32},{64,48},{80,64},{96,80},{112,96},{1... | collective-permute-start | bytes 22020104 | tf_op jit(solution)/shard_map/ppermute | solution.py:10
  115.4 4.8 %copy-start.1 = (bf16[32,8,4096]{2,1,0:T(8,128)(2,1)S(1)}, bf16[32,8,4096]{2,1,0:T(8,128)(2,1)}, u32[]{:S(2)}) copy-start(bf16[32,8,4096]{2,1,0:T(8,128)(2,1)} %all-gather.7.cloned.1.call-done) | copy-start | bytes 6291460
  115.4 9.4 %slice-start = ((s8[7340032]{0:T(1024)(128)(4,1)}), s8[4194304]{0:T(1024)(128)(4,1)S(1)}, s32[]{:S(2)}) async-start(s8[7340032]{0:T(1024)(128)(4,1)} %bitcast.157), calls=%async_computation.5 | async-start | bytes 8388608
  120.2 4.6 %copy-start.2 = (bf16[32,8,4096]{2,1,0:T(8,128)(2,1)S(1)}, bf16[32,8,4096]{2,1,0:T(8,128)(2,1)}, u32[]{:S(2)}) copy-start(bf16[32,8,4096]{2,1,0:T(8,128)(2,1)} %all-gather.5.cloned.1.call-done) | copy-start | bytes 6291460
  120.2 4.7 %slice-start.1 = ((s8[7340032]{0:T(1024)(128)(4,1)}), s8[3145728]{0:T(1024)(128)(4,1)S(1)}, s32[]{:S(2)}) async-start(s8[7340032]{0:T(1024)(128)(4,1)} %bitcast.157), calls=%async_computation.6 | async-start | bytes 6291456
  185.2 9.3 %slice-start.2 = ((s8[7340032]{0:T(1024)(128)(4,1)}), s8[4194304]{0:T(1024)(128)(4,1)S(1)}, s32[]{:S(2)}) async-start(s8[7340032]{0:T(1024)(128)(4,1)} %bitcast.159), calls=%async_computation.7 | async-start | bytes 8388608
  189.8 4.7 %slice-start.3 = ((s8[7340032]{0:T(1024)(128)(4,1)}), s8[3145728]{0:T(1024)(128)(4,1)S(1)}, s32[]{:S(2)}) async-start(s8[7340032]{0:T(1024)(128)(4,1)} %bitcast.159), calls=%async_computation.8 | async-start | bytes 6291456
  272.0 8.2 %copy-start.3 = (bf16[4096,8]{0,1:T(8,128)(2,1)S(1)}, bf16[4096,8]{0,1:T(8,128)(2,1)}, u32[]{:S(2)}) copy-start(bf16[4096,8]{0,1:T(8,128)(2,1)} %param.7) | copy-start | bytes 196612
  272.0 74.0 %all-to-all-start.1 = ((bf16[16,16,2,4096]{3,1,2,0:T(8,128)(2,1)}), bf16[16,16,2,4096]{3,1,2,0:T(8,128)(2,1)}, u32[]{:S(2)}, u32[]{:S(2)}) async-start(bf16[16,16,2,4096]{3,1,2,0:T(8,128)(2,1)} %copy.121), calls=%async_computation.1 | async-start | bytes 8388608 | tf_op jit(solution)/shard_map/all_to_all | solution.py:37
  349.9 10.3 %all-to-all-start.2 = ((bf16[8,2,2,4096]{3,2,1,0:T(2,128)(2,1)}), bf16[8,2,2,4096]{3,2,1,0:T(2,128)(2,1)S(1)}, u32[]{:S(2)}, u32[]{:S(2)}) async-start(bf16[8,2,2,4096]{3,2,1,0:T(2,128)(2,1)} %bitcast.36), calls=%async_computation.2 | async-start | bytes 524288 | tf_op jit(solution)/shard_map/all_to_all | solution.py:90
Sparse Core Ops, SparseCore 0:
  24.5 44.3 all-gather.6
  71.1 44.2 all-gather.4
where the time goes:
time: 371 us
  waiting for transfers between devices  271 us (73%)
  matrix products  41.4 us (11%)
  starting transfers between devices  14.3 us (4%)
  between operations  13.8 us (4%)
  blocking collectives  12.1 us (3%)
  local copies, waits for them, and re-layouts  11.3 us (3%)
  other arithmetic  6.56 us (2%)
    ppermute x3, waiting for transfers between devices, from_behind(): return lax.ppermute(value, axis, pairs)  117 us
    all_gather x2, waiting for transfers between devices, work_in_pieces(): gathered.append(jax.vmap(apply)(lax.all_gather(share, axis), starts))  83 us
    all_to_all x1, waiting for transfers between devices, sum_at_owner(): blocks = lax.all_to_all(split_up(x, dim, devices), axis, 0, 0, tiled=True)  64.8 us
    dot_general x4, matrix products, swiglu(): gate = jnp.dot(rows, gate_m, preferred_element_type=jnp.float32)  18.2 us
    dot_general x4, matrix products, swiglu(): up = jnp.dot(rows, up_m, preferred_element_type=jnp.float32)  14.9 us
    all_to_all x1, blocking collectives, shards(): lax.all_to_all(sending, 'expert', split_axis=1, concat_axis=1, tiled=True)  12.1 us
    all_to_all x1, starting transfers between devices, sum_at_owner(): blocks = lax.all_to_all(split_up(x, dim, devices), axis, 0, 0, tiled=True)  7.95 us
  transfers between devices with their start and end apart: 7, of which 6 were waited for; matrix products, arithmetic and copies ran while one was open for 10% of the time, Pallas kernels for 0%

commit v1 on v0

--- a/solution.py
+++ b/solution.py
@@ -2,6 +2,13 @@
 import jax.numpy as jnp
 from jax import lax
 from jax.sharding import PartitionSpec as P
+
+pairs_all_show = lambda u_in: jnp.concatenate(
+    lax.all_to_all(
+        jnp.stack(jnp.split(u_in, lax.axis_size("expert"), axis=1), axis=0), "expert", 0, 0
+    ),
+    axis=1,
+)
 
 
 def from_behind(value, axis, steps):
@@ -63,7 +70,7 @@
     even_rows = outgoing[:, :, 0]
     odd_rows = jnp.roll(outgoing[:, :, 1], -1, axis=0)
     sending = jnp.stack([even_rows, odd_rows], axis=0)
-    arrived = lax.all_to_all(sending, "expert", split_axis=1, concat_axis=1, tiled=True)
+    arrived = pairs_all_show(sending)
     arrived = arrived.reshape(2, n_experts * half_slots, width)
     gate_w = w_gate[0]
     up_w = w_up[0]

time: 371 us -> 372 us (level)
  no operation moved by 1% of the time
where the time goes in v1:
time: 372 us; the launch traced here: 371 us
  waiting for transfers between devices  271 us (73%)
  matrix products  41.4 us (11%)
  starting transfers between devices  14.3 us (4%)
  between operations  13.8 us (4%)
  blocking collectives  12.1 us (3%)
  local copies, waits for them, and re-layouts  11.5 us (3%)
  other arithmetic  7.11 us (2%)
    ppermute x3, waiting for transfers between devices, from_behind(): return lax.ppermute(value, axis, pairs)  117 us
    all_gather x2, waiting for transfers between devices, work_in_pieces(): gathered.append(jax.vmap(apply)(lax.all_gather(share, axis), starts))  83 us
    all_to_all x1, waiting for transfers between devices, sum_at_owner(): blocks = lax.all_to_all(split_up(x, dim, devices), axis, 0, 0, tiled=True)  64.8 us
    dot_general x4, matrix products, swiglu(): gate = jnp.dot(rows, gate_m, preferred_element_type=jnp.float32)  18.2 us
    dot_general x4, matrix products, swiglu(): up = jnp.dot(rows, up_m, preferred_element_type=jnp.float32)  14.9 us
    all_to_all x1, blocking collectives, lax.all_to_all(jnp.stack(jnp.split(u_in, lax.axis_size('expert'), axis=1)...  12.1 us
    all_to_all x1, starting transfers between devices, sum_at_owner(): blocks = lax.all_to_all(split_up(x, dim, devices), axis, 0, 0, tiled=True)  7.95 us
  transfers between devices with their start and end apart: 7, of which 6 were waited for; matrix products, arithmetic and copies ran while one was open for 10% of the time, Pallas kernels for 0%

profile of v1, /device:TPU:1, one launch (start us, length us, event | category | flops | bytes accessed | tf_op | source)
XLA Modules:
  0.0 371.4 jit_solution(15291652771396892532)
XLA Ops:
  6.5 0.7 broadcast_multiply_fusion
  7.3 0.8 copy.293
  8.7 1.2 scatter_custom_fusion
  11.9 12.1 %all_to_all.15 = bf16[8,2,1,2,4096]{4,3,1,2,0:T(2,128)(2,1)S(1)} all-to-all(bf16[8,2,1,2,4096]{4,3,1,2,0:T(2,128)(2,1)S(1)} %bitcast_dynamic-update-slice_fusion), channel_id=1, replica_groups=mesh['expert'=8,'shard'=16] {'expert'}, dimensions={0} | all-to-all | bytes 524288 | tf_op jit(solution)/shard_map/all_to_all | solution.py:7
  24.4 0.7 copy.307
  25.4 1.1 collective-permute-start
  26.7 0.7 copy.304
  27.5 1.1 collective-permute-start.2
  28.5 41.2 %all-gather.7.cloned.1.call-done = bf16[32,8,4096]{2,1,0:T(8,128)(2,1)} async-done(((bf16[2,8,4096]{2,1,0:T(8,128)(2,1)}), bf16[32,8,4096]{2,1,0:T(8,128)(2,1)}) %all-gather.7.cloned.1.call-update) | async-done | bytes 2097168 | tf_op jit(solution)/shard_map/all_gather | solution.py:33
  69.8 4.7 %fusion.16 = f32[16,8,896]{2,1,0:T(8,128)S(1)} fusion(bf16[1,4096,896]{2,1,0:T(8,128)(2,1)} %param.9, bf16[16,2,8,4096]{3,2,1,0:T(8,128)(2,1)} %bitcast.157), kind=kOutput, calls=%fused_computation.20 | convolution fusion | flops 939524096 | bytes 8847360 | tf_op jit(solution)/shard_map/vmap()/dot_general | solution.py:83
  74.4 41.8 %all-gather.5.cloned.1.call-done = bf16[32,8,4096]{2,1,0:T(8,128)(2,1)} async-done(((bf16[2,8,4096]{2,1,0:T(8,128)(2,1)}), bf16[32,8,4096]{2,1,0:T(8,128)(2,1)}) %all-gather.5.cloned.1.call-update) | async-done | bytes 2097168 | tf_op jit(solution)/shard_map/all_gather | solution.py:33
  116.2 4.8 %fusion.18 = f32[16,8,896]{2,1,0:T(8,128)S(1)} fusion(bf16[1,4096,896]{2,1,0:T(8,128)(2,1)} %param.9, bf16[16,2,8,4096]{3,2,1,0:T(8,128)(2,1)} %bitcast.161), kind=kOutput, calls=%fused_computation.22 | convolution fusion | flops 939524096 | bytes 8847360 | tf_op jit(solution)/shard_map/vmap()/dot_general | solution.py:83
  121.1 4.5 %fusion.47 = bf16[16,8,1,896]{3,1,0,2:T(8,128)(2,1)S(1)} fusion(bf16[1,4096,896]{2,1,0:T(8,128)(2,1)} %param.10, bf16[16,2,8,4096]{3,2,1,0:T(8,128)(2,1)S(1)} %bitcast.158, f32[16,8,896]{2,1,0:T(8,128)S(1)} %fusion.16), kind=kOutput, calls=%fused_computation.34 | convolution fusion | flops 940212224 | bytes 9076736 | tf_op jit(solution)/shard_map/vmap()/dot_general | solution.py:84
  125.7 1.3 fusion.44
  127.0 4.4 %fusion.8 = f32[16,8,896]{2,1,0:T(8,128)S(1)} fusion(bf16[1,4096,896]{2,1,0:T(8,128)(2,1)} %collective-permute-done, bf16[16,2,8,4096]{3,2,1,0:T(8,128)(2,1)S(1)} %bitcast.159), kind=kOutput, calls=%fused_computation.12 | convolution fusion | flops 939524096 | bytes 8847360 | tf_op jit(solution)/shard_map/vmap()/dot_general | solution.py:83
  131.4 4.4 %fusion.10 = f32[16,8,896]{2,1,0:T(8,128)S(1)} fusion(bf16[1,4096,896]{2,1,0:T(8,128)(2,1)} %collective-permute-done, bf16[16,2,8,4096]{3,2,1,0:T(8,128)(2,1)S(1)} %bitcast.163), kind=kOutput, calls=%fused_computation.14 | convolution fusion | flops 939524096 | bytes 8847360 | tf_op jit(solution)/shard_map/vmap()/dot_general | solution.py:83
  135.8 50.3 %collective-permute-done.1 = bf16[1,4096,896]{2,1,0:T(8,128)(2,1)} collective-permute-done((bf16[1,4096,896]{2,1,0:T(8,128)(2,1)}, bf16[1,4096,896]{2,1,0:T(8,128)(2,1)}, u32[]{:S(2)}, u32[]{:S(2)}) %collective-permute-start.1) | collective-permute-done | bytes 7340064 | tf_op jit(solution)/shard_map/ppermute | solution.py:17
  186.0 4.5 %fusion.51 = bf16[16,8,1,896]{3,1,0,2:T(8,128)(2,1)S(1)} fusion(f32[16,8,896]{2,1,0:T(8,128)S(1)} %fusion.8, bf16[1,4096,896]{2,1,0:T(8,128)(2,1)} %collective-permute-done.1, bf16[16,2,8,4096]{3,2,1,0:T(8,128)(2,1)S(1)} %bitcast.160), kind=kOutput, calls=%fused_computation.59 | convolution fusion | flops 940212224 | bytes 9076736 | tf_op jit(solution)/shard_map/vmap()/dot_general | solution.py:84
  190.6 4.5 %fusion.50 = bf16[16,8,1,896]{3,1,0,2:T(8,128)(2,1)S(1)} fusion(f32[16,8,896]{2,1,0:T(8,128)S(1)} %fusion.10, bf16[1,4096,896]{2,1,0:T(8,128)(2,1)} %collective-permute-done.1, bf16[16,2,8,4096]{3,2,1,0:T(8,128)(2,1)S(1)} %bitcast.164), kind=kOutput, calls=%fused_computation.58 | convolution fusion | flops 940212224 | bytes 9076736 | tf_op jit(solution)/shard_map/vmap()/dot_general | solution.py:84
  195.3 2.6 fusion.29
  198.0 66.7 %collective-permute-done.2 = bf16[1,896,4096]{2,1,0:T(8,128)(2,1)} collective-permute-done((bf16[1,896,4096]{2,1,0:T(8,128)(2,1)}, bf16[1,896,4096]{2,1,0:T(8,128)(2,1)}, u32[]{:S(2)}, u32[]{:S(2)}) %collective-permute-start.2) | collective-permute-done | bytes 7340064 | tf_op jit(solution)/shard_map/ppermute | solution.py:17
  264.7 5.5 %fusion.26 = bf16[16,16,1,4096]{3,1,0,2:T(8,128)(2,1)S(1)} fusion(bf16[16,16,896]{2,1,0:T(8,128)(2,1)S(1)} %bitcast.171, bf16[1,896,4096]{2,1,0:T(8,128)(2,1)} %collective-permute-done.2), kind=kOutput, calls=%fused_computation.26 | convolution fusion | flops 1880096768 | bytes 9895936 | tf_op jit(solution)/shard_map/dot_general | solution.py:94
  270.6 2.3 copy.310
  272.8 8.0 %all-to-all-start.1 = ((bf16[16,16,2,4096]{3,1,2,0:T(8,128)(2,1)}), bf16[16,16,2,4096]{3,1,2,0:T(8,128)(2,1)}, u32[]{:S(2)}, u32[]{:S(2)}) async-start(bf16[16,16,2,4096]{3,1,2,0:T(8,128)(2,1)} %copy.310), calls=%async_computation.1 | async-start | bytes 8388608 | tf_op jit(solution)/shard_map/all_to_all | solution.py:44
  281.2 0.7 gather_fusion.1
  282.0 64.8 %all-to-all-done.1 = bf16[16,16,2,4096]{3,1,2,0:T(8,128)(2,1)} async-done(((bf16[16,16,2,4096]{3,1,2,0:T(8,128)(2,1)}), bf16[16,16,2,4096]{3,1,2,0:T(8,128)(2,1)}, u32[]{:S(2)}, u32[]{:S(2)}) %all-to-all-start.1) | async-done | bytes 4194336 | tf_op jit(solution)/shard_map/all_to_all | solution.py:44
  346.8 3.0 reduce_sum.34
  349.8 1.0 copy.312
  350.8 3.8 %all-to-all-start.2 = ((bf16[8,2,2,4096]{3,2,1,0:T(2,128)(2,1)}), bf16[8,2,2,4096]{3,2,1,0:T(2,128)(2,1)S(1)}, u32[]{:S(2)}, u32[]{:S(2)}) async-start(bf16[8,2,2,4096]{3,2,1,0:T(2,128)(2,1)} %bitcast.37), calls=%async_computation.2 | async-start | bytes 524288 | tf_op jit(solution)/shard_map/all_to_all | solution.py:97
  354.7 6.3 %all-to-all-done.2 = bf16[8,2,2,4096]{3,2,1,0:T(2,128)(2,1)S(1)} async-done(((bf16[8,2,2,4096]{3,2,1,0:T(2,128)(2,1)}), bf16[8,2,2,4096]{3,2,1,0:T(2,128)(2,1)S(1)}, u32[]{:S(2)}, u32[]{:S(2)}) %all-to-all-start.2) | async-done | bytes 262176 | tf_op jit(solution)/shard_map/all_to_all | solution.py:97
  362.7 0.6 gather_fusion
  363.6 1.0 multiply_reduce_fusion
  (74 shorter events, 6.6 us)
Async XLA Ops:
  6.5 2.1 copy-start
  6.5 63.2 %all-gather.7.cloned.1.call-start = ((), (), s32[]{:S(2)}) async-start(), calls=%async_computation.4 | async-start | bytes 2228224 | tf_op jit(solution)/shard_map/all_gather | solution.py:33
  25.2 91.0 %all-gather.5.cloned.1.call-start = ((), (), s32[]{:S(2)}) async-start(), calls=%async_computation.3 | async-start | bytes 2228224 | tf_op jit(solution)/shard_map/all_gather | solution.py:33
  25.4 101.6 %collective-permute-start = (bf16[1,4096,896]{2,1,0:T(8,128)(2,1)}, bf16[1,4096,896]{2,1,0:T(8,128)(2,1)}, u32[]{:S(2)}, u32[]{:S(2)}) collective-permute-start(bf16[1,4096,896]{2,1,0:T(8,128)(2,1)} %param.9), channel_id=1, source_target_pairs={{0,112},{16,0},{32,16},{48,32},{64,48},{80,64},{96,80},{112,96},{1... | collective-permute-start | bytes 22020104 | tf_op jit(solution)/shard_map/ppermute | solution.py:17
  26.5 159.6 %collective-permute-start.1 = (bf16[1,4096,896]{2,1,0:T(8,128)(2,1)}, bf16[1,4096,896]{2,1,0:T(8,128)(2,1)}, u32[]{:S(2)}, u32[]{:S(2)}) collective-permute-start(bf16[1,4096,896]{2,1,0:T(8,128)(2,1)} %param.10), channel_id=1, source_target_pairs={{0,112},{16,0},{32,16},{48,32},{64,48},{80,64},{96,80},{112,96},{1... | collective-permute-start | bytes 22020104 | tf_op jit(solution)/shard_map/ppermute | solution.py:17
  27.5 237.2 %collective-permute-start.2 = (bf16[1,896,4096]{2,1,0:T(8,128)(2,1)}, bf16[1,896,4096]{2,1,0:T(8,128)(2,1)}, u32[]{:S(2)}, u32[]{:S(2)}) collective-permute-start(bf16[1,896,4096]{2,1,0:T(8,128)(2,1)} %param.11), channel_id=1, source_target_pairs={{0,112},{16,0},{32,16},{48,32},{64,48},{80,64},{96,80},{112,96},{1... | collective-permute-start | bytes 22020104 | tf_op jit(solution)/shard_map/ppermute | solution.py:17
  116.2 4.8 %copy-start.1 = (bf16[32,8,4096]{2,1,0:T(8,128)(2,1)S(1)}, bf16[32,8,4096]{2,1,0:T(8,128)(2,1)}, u32[]{:S(2)}) copy-start(bf16[32,8,4096]{2,1,0:T(8,128)(2,1)} %all-gather.7.cloned.1.call-done) | copy-start | bytes 6291460
  116.2 9.4 %slice-start = ((s8[7340032]{0:T(1024)(128)(4,1)}), s8[4194304]{0:T(1024)(128)(4,1)S(1)}, s32[]{:S(2)}) async-start(s8[7340032]{0:T(1024)(128)(4,1)} %bitcast.175), calls=%async_computation.5 | async-start | bytes 8388608
  121.0 4.6 %copy-start.2 = (bf16[32,8,4096]{2,1,0:T(8,128)(2,1)S(1)}, bf16[32,8,4096]{2,1,0:T(8,128)(2,1)}, u32[]{:S(2)}) copy-start(bf16[32,8,4096]{2,1,0:T(8,128)(2,1)} %all-gather.5.cloned.1.call-done) | copy-start | bytes 6291460
  121.0 4.7 %slice-start.1 = ((s8[7340032]{0:T(1024)(128)(4,1)}), s8[3145728]{0:T(1024)(128)(4,1)S(1)}, s32[]{:S(2)}) async-start(s8[7340032]{0:T(1024)(128)(4,1)} %bitcast.175), calls=%async_computation.6 | async-start | bytes 6291456
  186.0 9.3 %slice-start.2 = ((s8[7340032]{0:T(1024)(128)(4,1)}), s8[4194304]{0:T(1024)(128)(4,1)S(1)}, s32[]{:S(2)}) async-start(s8[7340032]{0:T(1024)(128)(4,1)} %bitcast.177), calls=%async_computation.7 | async-start | bytes 8388608
  190.6 4.7 %slice-start.3 = ((s8[7340032]{0:T(1024)(128)(4,1)}), s8[3145728]{0:T(1024)(128)(4,1)S(1)}, s32[]{:S(2)}) async-start(s8[7340032]{0:T(1024)(128)(4,1)} %bitcast.177), calls=%async_computation.8 | async-start | bytes 6291456
  272.8 8.2 %copy-start.3 = (bf16[4096,8]{0,1:T(8,128)(2,1)S(1)}, bf16[4096,8]{0,1:T(8,128)(2,1)}, u32[]{:S(2)}) copy-start(bf16[4096,8]{0,1:T(8,128)(2,1)} %param.7) | copy-start | bytes 196612
  272.8 74.0 %all-to-all-start.1 = ((bf16[16,16,2,4096]{3,1,2,0:T(8,128)(2,1)}), bf16[16,16,2,4096]{3,1,2,0:T(8,128)(2,1)}, u32[]{:S(2)}, u32[]{:S(2)}) async-start(bf16[16,16,2,4096]{3,1,2,0:T(8,128)(2,1)} %copy.310), calls=%async_computation.1 | async-start | bytes 8388608 | tf_op jit(solution)/shard_map/all_to_all | solution.py:44
  350.8 10.3 %all-to-all-start.2 = ((bf16[8,2,2,4096]{3,2,1,0:T(2,128)(2,1)}), bf16[8,2,2,4096]{3,2,1,0:T(2,128)(2,1)S(1)}, u32[]{:S(2)}, u32[]{:S(2)}) async-start(bf16[8,2,2,4096]{3,2,1,0:T(2,128)(2,1)} %bitcast.37), calls=%async_computation.2 | async-start | bytes 524288 | tf_op jit(solution)/shard_map/all_to_all | solution.py:97
Sparse Core Ops, SparseCore 0:
  25.3 44.3 all-gather.6
  71.9 44.2 all-gather.4
